TPU v7x, 32 devices: a whole 2x2x4 slice. The times are simulated.
32 devices in a mesh: groups: 2 (over y), gx: 4 (over z), gy: 2 (over x), gz: 2 (over core).
Axes of the slice: x: 2, y: 2, z: 4, core: 2. Of those that a mesh axis runs over, the one named last changes fastest.
Arguments:
- latents: bfloat16 [8, 2, 2, 128, 128], P(('groups', 'gx'), 'gy', 'gz'), parts along dimension 0, may hold values from -6 to 6
- offsets: bfloat16 [8, 2, 2, 3, 128], P(('groups', 'gx'), 'gy', 'gz'), parts along dimension 0, may hold values from 0 to 1
- neighbours: int32 [8, 2, 2, 384], P(('groups', 'gx'), 'gy', 'gz'), parts along dimension 0, may hold values from 0 to 2047, as said below
- counts: int32 [8, 2, 2], P(('groups', 'gx'), 'gy', 'gz'), parts along dimension 0, may hold values from 1 to 384, as said below
- w_recv: bfloat16 [1, 128, 128], replicated, may hold values from -0.5 to 0.5
- w_send: bfloat16 [1, 128, 128], replicated, may hold values from -0.5 to 0.5
- w_rel: bfloat16 [1, 4, 128], replicated, may hold values from -3 to 3
- b_first: float32 [1, 128], replicated, may hold values from -5 to 5
- w_edge: bfloat16 [1, 128, 128], replicated, may hold values from -0.5 to 0.5
- b_edge: float32 [1, 128], replicated, may hold values from -5 to 5
- w_self: bfloat16 [1, 128, 128], replicated, may hold values from -0.5 to 0.5
- w_agg: bfloat16 [1, 128, 128], replicated, may hold values from -0.5 to 0.5
- w_out: bfloat16 [1, 128, 128], replicated, may hold values from -0.5 to 0.5
- norm_gain: float32 [1, 128], replicated, may hold values from 0.1 to 1.9
Outputs:
- processed: bfloat16 [8, 2, 2, 128, 128], P(('groups', 'gx'), 'gy', 'gz'), parts along dimension 0
There are 2 independent parts, one for each index of `groups`. A program takes and returns all parts, laid end to end along the dimension named above; an argument that names none is the same for every part. Nothing has to cross between parts.
Inputs may be any that keep to these rules, and one draw needn't show every extreme that they name: `neighbours`: each sender is a particle of the same cell or of a cell whose three coordinates differ from the receiver cell's by at most one. Only the first counts[cell] senders of a cell are live, the rest is padding. In the cells whose first coordinate is below 1 all 384 senders are live.
All inputs are finite; a program needn't handle non-finite values.
Results may differ from a plain program's by a relative error of at most 0.0055.
Values may be sent and summed in bfloat16 or wider, within the bound.
A program may use at most 64 MiB of HBM per device.

v0:
```python
import jax
import jax.numpy as jnp
from jax import lax
from jax.sharding import PartitionSpec as P

SLOTS = 128


def extended(shard, sides, width):
    for axis, dim in sides:
        size, length = (lax.axis_size(axis), shard.shape[dim])
        up = [(i, (i + 1) % size) for i in range(size - 1)]
        down = [(j, i) for i, j in up]
        last = lax.slice_in_dim(shard, length - width, length, axis=dim)
        first = lax.slice_in_dim(shard, 0, width, axis=dim)
        before = lax.ppermute(last, axis, up)
        after = lax.ppermute(first, axis, down)
        shard = jnp.concatenate([before, shard, after], axis=dim)
    return shard


def edge_sum(recv_term, send_term, recv_place, send_place, live_mask, rel_weight, w_edge, b_edge):
    row_count, latent_width = recv_term.shape
    tile_rows = min(16, row_count)
    tile_count = row_count // tile_rows

    def tile_messages(operands):
        recv_tile, place_tile = operands
        relative = send_place[:, None, :] - place_tile[:, :, None]
        features = jnp.concatenate(
            [relative, 0.25 * jnp.sum(relative * relative, axis=0, keepdims=True)], axis=0
        )
        place_term = jnp.einsum(
            "cij,cw->ijw", features, rel_weight, precision=lax.Precision.HIGHEST
        )
        pre_act = recv_tile[:, None, :] + send_term[None, :, :] + place_term
        edge_act = jax.nn.silu(pre_act).astype(jnp.bfloat16)
        message = (
            jnp.dot(edge_act.reshape(-1, latent_width), w_edge, preferred_element_type=jnp.float32)
            + b_edge
        )
        message = jax.nn.silu(message).reshape(tile_rows, -1, latent_width)
        return jnp.einsum("ijw,j->iw", message, live_mask, precision=lax.Precision.HIGHEST)

    recv_tiles = recv_term.reshape(tile_count, tile_rows, latent_width)
    place_tiles = recv_place.reshape(3, tile_count, tile_rows).transpose(1, 0, 2)
    return lax.map(tile_messages, (recv_tiles, place_tiles)).reshape(row_count, latent_width)


def renew(latent, summed, w_self, w_agg, w_out, norm_gain):
    pooled = (summed / latent.shape[0]).astype(jnp.bfloat16)
    hidden = jax.nn.silu(
        jnp.dot(latent, w_self, preferred_element_type=jnp.float32)
        + jnp.dot(pooled, w_agg, preferred_element_type=jnp.float32)
    ).astype(jnp.bfloat16)
    result = jnp.dot(hidden, w_out, preferred_element_type=jnp.float32)
    center = jnp.mean(result, axis=-1, keepdims=True)
    spread = jnp.mean((result - center) ** 2, axis=-1, keepdims=True)
    normed = (result - center) * lax.rsqrt(spread + 1e-05) * norm_gain
    return (latent.astype(jnp.float32) + normed).astype(jnp.bfloat16)


def widen(field):
    collected = lax.all_gather(field, "gy", axis=1, tiled=True)
    collected = lax.all_gather(collected, "gz", axis=2, tiled=True)
    return extended(collected, (("gx", 0),), 1)


def shards(
    latents,
    offsets,
    neighbours,
    counts,
    w_recv,
    w_send,
    w_rel,
    b_first,
    w_edge,
    b_edge,
    w_self,
    w_agg,
    w_out,
    norm_gain,
):
    span_x, span_y, span_z = (latents.shape[0], latents.shape[1], latents.shape[2])
    latent_width = latents.shape[4]
    cell_count = span_x * span_y * span_z
    index_x = lax.axis_index("gx")
    index_y = lax.axis_index("gy")
    index_z = lax.axis_index("gz")
    whole_y = span_y * lax.axis_size("gy")
    whole_z = span_z * lax.axis_size("gz")
    base_x = index_x * span_x - 1
    ext_rows = (span_x + 2) * whole_y * whole_z * SLOTS
    cell_of = neighbours // SLOTS
    slot_of = neighbours % SLOTS
    coord_z = cell_of % whole_z
    coord_y = cell_of // whole_z % whole_y
    coord_x = cell_of // (whole_y * whole_z)
    local_ids = (
        (((coord_x - base_x) * whole_y + coord_y) * whole_z + coord_z) * SLOTS + slot_of
    ).reshape(cell_count, -1)
    sender_coords = (
        jnp.stack([coord_x, coord_y, coord_z], axis=-2)
        .astype(jnp.float32)
        .reshape(cell_count, 3, -1)
    )
    grid_x = (index_x * span_x + lax.iota(jnp.int32, span_x))[:, None, None]
    grid_y = (index_y * span_y + lax.iota(jnp.int32, span_y))[None, :, None]
    grid_z = (index_z * span_z + lax.iota(jnp.int32, span_z))[None, None, :]
    own_coords = jnp.stack([grid_x, grid_y, grid_z], axis=-1).astype(jnp.float32)
    own_places = (offsets.astype(jnp.float32) + own_coords[..., None]).reshape(cell_count, 3, SLOTS)
    rim_offsets = widen(offsets)
    offset_table = rim_offsets.transpose(3, 0, 1, 2, 4).reshape(3, ext_rows)
    count_rows = counts.reshape(cell_count)
    blocks_needed = (count_rows + SLOTS - 1) // SLOTS
    slot_ids = lax.iota(jnp.int32, SLOTS)
    current = latents.reshape(cell_count, SLOTS, latent_width)
    step_index = 0
    rimmed = widen(current.reshape(span_x, span_y, span_z, SLOTS, latent_width)).reshape(
        ext_rows, latent_width
    )
    rel_weight = w_rel[step_index].astype(jnp.float32)

    def senders(cell_index, block_index, rimmed=rimmed, step_index=step_index):
        sender_ids = lax.dynamic_slice_in_dim(local_ids[cell_index], block_index * SLOTS, SLOTS)
        gathered = jnp.take(rimmed, sender_ids, axis=0)
        send_term = jnp.dot(gathered, w_send[step_index], preferred_element_type=jnp.float32)
        send_place = jnp.take(offset_table, sender_ids, axis=1).astype(
            jnp.float32
        ) + lax.dynamic_slice_in_dim(sender_coords[cell_index], block_index * SLOTS, SLOTS, axis=1)
        live_mask = (block_index * SLOTS + slot_ids < count_rows[cell_index]).astype(jnp.float32)
        return (send_term, send_place, live_mask)

    def block_sum(
        cell_index,
        recv_term,
        first_block,
        last_block,
        step_index=step_index,
        rel_weight=rel_weight,
        senders=senders,
    ):

        def add_block(block_index, summed):
            send_term, send_place, live_mask = senders(cell_index, block_index)
            return summed + edge_sum(
                recv_term,
                send_term,
                own_places[cell_index],
                send_place,
                live_mask,
                rel_weight,
                w_edge[step_index],
                b_edge[step_index],
            )

        return lax.fori_loop(
            first_block, last_block, add_block, jnp.zeros((SLOTS, latent_width), jnp.float32)
        )

    recv_terms = (
        jnp.dot(
            current.reshape(-1, latent_width),
            w_recv[step_index],
            preferred_element_type=jnp.float32,
        )
        + b_first[step_index]
    ).reshape(cell_count, SLOTS, latent_width)
    sums = block_sum(0, recv_terms[0], 0, blocks_needed[0])
    current = jnp.stack(
        [
            renew(
                current[0],
                sums,
                w_self[step_index],
                w_agg[step_index],
                w_out[step_index],
                norm_gain[step_index],
            )
        ]
    )
    return current.reshape(span_x, span_y, span_z, SLOTS, latent_width)


def solution(mesh):
    in_specs = (
        P(("groups", "gx"), "gy", "gz", None, None),
        P(("groups", "gx"), "gy", "gz", None, None),
        P(("groups", "gx"), "gy", "gz", None),
        P(("groups", "gx"), "gy", "gz"),
        P(),
        P(),
        P(),
        P(),
        P(),
        P(),
        P(),
        P(),
        P(),
        P(),
    )
    out_specs = P(("groups", "gx"), "gy", "gz", None, None)
    return jax.shard_map(shards, mesh=mesh, in_specs=in_specs, out_specs=out_specs, check_vma=False)
```

profile of v0, /device:TPU:0, one launch (start us, length us, event | category | flops | bytes accessed | tf_op | source)
XLA Modules:
  0.0 117.4 jit_solution(15140709854701901017)
XLA Ops:
  0.0 5.9 %all_gather.14 = bf16[1,2,1,128,128]{4,3,2,0,1:T(8,128)(2,1)S(1)} all-gather(bf16[1,1,1,128,128]{4,3,2,0,1:T(8,128)(2,1)} %bitcast.142), channel_id=1, replica_groups=mesh['groups'=2,'gx'=4,'gy'=2,'gz'=2] {'gy'}, dimensions={1}, use_global_device_ids=true | all-gather | bytes 98304 | tf_op jit(solution)/shard_map/all_gather | solution.py:64
  5.9 2.0 %all_gather.15 = bf16[1,2,2,128,128]{4,3,2,1,0:T(8,128)(2,1)S(1)} all-gather(bf16[1,2,1,128,128]{4,3,2,1,0:T(8,128)(2,1)S(1)} %bitcast.144), channel_id=1, replica_groups=mesh['groups'=2,'gx'=4,'gy'=2,'gz'=2] {'gz'}, dimensions={2}, use_global_device_ids=true | all-gather | bytes 196608 | tf_op jit(solution)/shard_map/all_gather | solution.py:65
  7.9 4.1 %collective-permute-start.2 = (bf16[1,2,2,128,128]{4,3,2,1,0:T(8,128)(2,1)S(1)}, bf16[1,2,2,128,128]{4,3,2,1,0:T(8,128)(2,1)S(1)}, u32[]{:S(2)}, u32[]{:S(2)}) collective-permute-start(bf16[1,2,2,128,128]{4,3,2,1,0:T(8,128)(2,1)S(1)} %all_gather.15), channel_id=1, source_target_pairs={{0,4},{4,8},{8,12},{1,5},{5,9},{9,13},{2,6},{6,10},{10,14},{3,7},{... | collective-permute-start | bytes 393224 | tf_op jit(solution)/shard_map/ppermute | solution.py:16
  12.0 1.3 %collective-permute-start.3 = (bf16[1,2,2,128,128]{4,3,2,1,0:T(8,128)(2,1)S(1)}, bf16[1,2,2,128,128]{4,3,2,1,0:T(8,128)(2,1)S(1)}, u32[]{:S(2)}, u32[]{:S(2)}) collective-permute-start(bf16[1,2,2,128,128]{4,3,2,1,0:T(8,128)(2,1)S(1)} %all_gather.15), channel_id=1, source_target_pairs={{4,0},{8,4},{12,8},{5,1},{9,5},{13,9},{6,2},{10,6},{14,10},{7,3},{... | collective-permute-start | bytes 393224 | tf_op jit(solution)/shard_map/ppermute | solution.py:17
  13.4 4.2 %all_gather.12 = bf16[1,2,1,3,128]{4,3,2,0,1:T(4,128)(2,1)S(1)} all-gather(bf16[1,1,1,3,128]{4,3,2,0,1:T(4,128)(2,1)S(1)} %bitcast.147), channel_id=1, replica_groups=mesh['groups'=2,'gx'=4,'gy'=2,'gz'=2] {'gy'}, dimensions={1}, use_global_device_ids=true | all-gather | bytes 2304 | tf_op jit(solution)/shard_map/all_gather | solution.py:64
  17.6 1.8 %all_gather.13 = bf16[1,2,2,3,128]{4,3,2,0,1:T(4,128)(2,1)S(1)} all-gather(bf16[1,2,1,3,128]{4,3,2,0,1:T(4,128)(2,1)S(1)} %all_gather.12), channel_id=1, replica_groups=mesh['groups'=2,'gx'=4,'gy'=2,'gz'=2] {'gz'}, dimensions={2}, use_global_device_ids=true | all-gather | bytes 4608 | tf_op jit(solution)/shard_map/all_gather | solution.py:65
  19.4 4.5 %collective-permute-start = (bf16[1,2,2,3,128]{4,3,2,0,1:T(4,128)(2,1)S(1)}, bf16[1,2,2,3,128]{4,3,2,0,1:T(4,128)(2,1)S(1)}, u32[]{:S(2)}, u32[]{:S(2)}) collective-permute-start(bf16[1,2,2,3,128]{4,3,2,0,1:T(4,128)(2,1)S(1)} %all_gather.13), channel_id=1, source_target_pairs={{0,4},{4,8},{8,12},{1,5},{5,9},{9,13},{2,6},{6,10},{10,14},{3,7},{... | collective-permute-start | bytes 9224 | tf_op jit(solution)/shard_map/ppermute | solution.py:16
  23.9 1.3 %collective-permute-start.1 = (bf16[1,2,2,3,128]{4,3,2,0,1:T(4,128)(2,1)S(1)}, bf16[1,2,2,3,128]{4,3,2,0,1:T(4,128)(2,1)S(1)}, u32[]{:S(2)}, u32[]{:S(2)}) collective-permute-start(bf16[1,2,2,3,128]{4,3,2,0,1:T(4,128)(2,1)S(1)} %all_gather.13), channel_id=1, source_target_pairs={{4,0},{8,4},{12,8},{5,1},{9,5},{13,9},{6,2},{10,6},{14,10},{7,3},{... | collective-permute-start | bytes 9224 | tf_op jit(solution)/shard_map/ppermute | solution.py:17
  27.9 1.6 %collective-permute-done.1 = bf16[1,2,2,3,128]{4,3,2,0,1:T(4,128)(2,1)S(1)} collective-permute-done((bf16[1,2,2,3,128]{4,3,2,0,1:T(4,128)(2,1)S(1)}, bf16[1,2,2,3,128]{4,3,2,0,1:T(4,128)(2,1)S(1)}, u32[]{:S(2)}, u32[]{:S(2)}) %collective-permute-start.1) | collective-permute-done | bytes 3104 | tf_op jit(solution)/shard_map/ppermute | solution.py:17
  29.9 0.7 copy-done.1
  30.6 85.0 %while.23 = (s32[]{:T(128)}, f32[128,128]{1,0:T(8,128)S(1)}, s32[]{:T(128)}, f32[128,128]{1,0:T(8,128)S(1)}, f32[1,1,1,3,128]{4,3,2,1,0:T(4,128)S(1)}, /*index=5...) while((s32[]{:T(128)}, f32[128,128]{1,0:T(8,128)S(1)}, ...), condition=%wide.region_4.5_spmd.clone, body=%wide.region_0.4_spmd.clone.sunk | while | flops 90240648 | bytes 3800472 | solution.py:158
  30.6 0.7 gather_fusion.1
  31.6 0.7 gather_fusion
  32.5 0.7 compare_convert_fusion.2
  33.3 25.6 %while.24 = (s32[]{:T(128)}, f32[8,16,128]{2,1,0:T(8,128)S(1)}, f32[8,16,128]{2,1,0:T(8,128)S(1)}, f32[128,128]{1,0:T(8,128)S(1)}, f32[3,128]{1,0:T(4,128)S(1)},...) while((s32[]{:T(128)}, f32[8,16,128]{2,1,0:T(8,128)S(1)}, ...), condition=%wide.region_3.3_spmd, body=%wide.region_1.2_spmd.sunk | while | flops 86009856 | bytes 3381177 | solution.py:47
  33.5 1.8 %multiply_convert_fusion.8 = bf16[16,128,128]{2,1,0:T(8,128)(2,1)S(1)} fusion(f32[128,128]{1,0:T(8,128)S(1)} %get-tuple-element.507, f32[16,128]{1,0:T(8,128)S(1)} %dynamic-slice_bitcast_fusion.2, f32[1,16,128]{2,0,1:T(1,128)S(1)} %bitcast.138, f32[3,16,128]{2,0,1:T(4,128)S(1)} %get-tuple-element.481, f32[4,128]{1,0:T(4,128)S(1)} %get-tuple-element.510), kind=kOutput, calls=%fused_computation.6.clone.1 | convolution fusion | flops 14426112 | bytes 632832 | tf_op jit(solution)/shard_map/while/body/while/body/eval_jaxpr/cij,cw->ijw/dot_general | solution.py:33
  36.7 1.8 %multiply_convert_fusion.8 = bf16[16,128,128]{2,1,0:T(8,128)(2,1)S(1)} fusion(f32[128,128]{1,0:T(8,128)S(1)} %get-tuple-element.507, f32[16,128]{1,0:T(8,128)S(1)} %dynamic-slice_bitcast_fusion.2, f32[1,16,128]{2,0,1:T(1,128)S(1)} %bitcast.138, f32[3,16,128]{2,0,1:T(4,128)S(1)} %get-tuple-element.481, f32[4,128]{1,0:T(4,128)S(1)} %get-tuple-element.510), kind=kOutput, calls=%fused_computation.6.clone.1 | convolution fusion | flops 14426112 | bytes 632832 | tf_op jit(solution)/shard_map/while/body/while/body/eval_jaxpr/cij,cw->ijw/dot_general | solution.py:33
  39.9 1.8 %multiply_convert_fusion.8 = bf16[16,128,128]{2,1,0:T(8,128)(2,1)S(1)} fusion(f32[128,128]{1,0:T(8,128)S(1)} %get-tuple-element.507, f32[16,128]{1,0:T(8,128)S(1)} %dynamic-slice_bitcast_fusion.2, f32[1,16,128]{2,0,1:T(1,128)S(1)} %bitcast.138, f32[3,16,128]{2,0,1:T(4,128)S(1)} %get-tuple-element.481, f32[4,128]{1,0:T(4,128)S(1)} %get-tuple-element.510), kind=kOutput, calls=%fused_computation.6.clone.1 | convolution fusion | flops 14426112 | bytes 632832 | tf_op jit(solution)/shard_map/while/body/while/body/eval_jaxpr/cij,cw->ijw/dot_general | solution.py:33
  43.1 1.8 %multiply_convert_fusion.8 = bf16[16,128,128]{2,1,0:T(8,128)(2,1)S(1)} fusion(f32[128,128]{1,0:T(8,128)S(1)} %get-tuple-element.507, f32[16,128]{1,0:T(8,128)S(1)} %dynamic-slice_bitcast_fusion.2, f32[1,16,128]{2,0,1:T(1,128)S(1)} %bitcast.138, f32[3,16,128]{2,0,1:T(4,128)S(1)} %get-tuple-element.481, f32[4,128]{1,0:T(4,128)S(1)} %get-tuple-element.510), kind=kOutput, calls=%fused_computation.6.clone.1 | convolution fusion | flops 14426112 | bytes 632832 | tf_op jit(solution)/shard_map/while/body/while/body/eval_jaxpr/cij,cw->ijw/dot_general | solution.py:33
  46.3 1.8 %multiply_convert_fusion.8 = bf16[16,128,128]{2,1,0:T(8,128)(2,1)S(1)} fusion(f32[128,128]{1,0:T(8,128)S(1)} %get-tuple-element.507, f32[16,128]{1,0:T(8,128)S(1)} %dynamic-slice_bitcast_fusion.2, f32[1,16,128]{2,0,1:T(1,128)S(1)} %bitcast.138, f32[3,16,128]{2,0,1:T(4,128)S(1)} %get-tuple-element.481, f32[4,128]{1,0:T(4,128)S(1)} %get-tuple-element.510), kind=kOutput, calls=%fused_computation.6.clone.1 | convolution fusion | flops 14426112 | bytes 632832 | tf_op jit(solution)/shard_map/while/body/while/body/eval_jaxpr/cij,cw->ijw/dot_general | solution.py:33
  49.5 1.8 %multiply_convert_fusion.8 = bf16[16,128,128]{2,1,0:T(8,128)(2,1)S(1)} fusion(f32[128,128]{1,0:T(8,128)S(1)} %get-tuple-element.507, f32[16,128]{1,0:T(8,128)S(1)} %dynamic-slice_bitcast_fusion.2, f32[1,16,128]{2,0,1:T(1,128)S(1)} %bitcast.138, f32[3,16,128]{2,0,1:T(4,128)S(1)} %get-tuple-element.481, f32[4,128]{1,0:T(4,128)S(1)} %get-tuple-element.510), kind=kOutput, calls=%fused_computation.6.clone.1 | convolution fusion | flops 14426112 | bytes 632832 | tf_op jit(solution)/shard_map/while/body/while/body/eval_jaxpr/cij,cw->ijw/dot_general | solution.py:33
  52.7 1.8 %multiply_convert_fusion.8 = bf16[16,128,128]{2,1,0:T(8,128)(2,1)S(1)} fusion(f32[128,128]{1,0:T(8,128)S(1)} %get-tuple-element.507, f32[16,128]{1,0:T(8,128)S(1)} %dynamic-slice_bitcast_fusion.2, f32[1,16,128]{2,0,1:T(1,128)S(1)} %bitcast.138, f32[3,16,128]{2,0,1:T(4,128)S(1)} %get-tuple-element.481, f32[4,128]{1,0:T(4,128)S(1)} %get-tuple-element.510), kind=kOutput, calls=%fused_computation.6.clone.1 | convolution fusion | flops 14426112 | bytes 632832 | tf_op jit(solution)/shard_map/while/body/while/body/eval_jaxpr/cij,cw->ijw/dot_general | solution.py:33
  55.9 1.8 %multiply_convert_fusion.8 = bf16[16,128,128]{2,1,0:T(8,128)(2,1)S(1)} fusion(f32[128,128]{1,0:T(8,128)S(1)} %get-tuple-element.507, f32[16,128]{1,0:T(8,128)S(1)} %dynamic-slice_bitcast_fusion.2, f32[1,16,128]{2,0,1:T(1,128)S(1)} %bitcast.138, f32[3,16,128]{2,0,1:T(4,128)S(1)} %get-tuple-element.481, f32[4,128]{1,0:T(4,128)S(1)} %get-tuple-element.510), kind=kOutput, calls=%fused_computation.6.clone.1 | convolution fusion | flops 14426112 | bytes 632832 | tf_op jit(solution)/shard_map/while/body/while/body/eval_jaxpr/cij,cw->ijw/dot_general | solution.py:33
  58.9 0.7 gather_fusion.1
  59.9 0.7 gather_fusion
  60.9 0.7 compare_convert_fusion.2
  61.6 25.6 %while.24 = (s32[]{:T(128)}, f32[8,16,128]{2,1,0:T(8,128)S(1)}, f32[8,16,128]{2,1,0:T(8,128)S(1)}, f32[128,128]{1,0:T(8,128)S(1)}, f32[3,128]{1,0:T(4,128)S(1)},...) while((s32[]{:T(128)}, f32[8,16,128]{2,1,0:T(8,128)S(1)}, ...), condition=%wide.region_3.3_spmd, body=%wide.region_1.2_spmd.sunk | while | flops 86009856 | bytes 3381177 | solution.py:47
  61.8 1.8 %multiply_convert_fusion.8 = bf16[16,128,128]{2,1,0:T(8,128)(2,1)S(1)} fusion(f32[128,128]{1,0:T(8,128)S(1)} %get-tuple-element.507, f32[16,128]{1,0:T(8,128)S(1)} %dynamic-slice_bitcast_fusion.2, f32[1,16,128]{2,0,1:T(1,128)S(1)} %bitcast.138, f32[3,16,128]{2,0,1:T(4,128)S(1)} %get-tuple-element.481, f32[4,128]{1,0:T(4,128)S(1)} %get-tuple-element.510), kind=kOutput, calls=%fused_computation.6.clone.1 | convolution fusion | flops 14426112 | bytes 632832 | tf_op jit(solution)/shard_map/while/body/while/body/eval_jaxpr/cij,cw->ijw/dot_general | solution.py:33
  65.0 1.8 %multiply_convert_fusion.8 = bf16[16,128,128]{2,1,0:T(8,128)(2,1)S(1)} fusion(f32[128,128]{1,0:T(8,128)S(1)} %get-tuple-element.507, f32[16,128]{1,0:T(8,128)S(1)} %dynamic-slice_bitcast_fusion.2, f32[1,16,128]{2,0,1:T(1,128)S(1)} %bitcast.138, f32[3,16,128]{2,0,1:T(4,128)S(1)} %get-tuple-element.481, f32[4,128]{1,0:T(4,128)S(1)} %get-tuple-element.510), kind=kOutput, calls=%fused_computation.6.clone.1 | convolution fusion | flops 14426112 | bytes 632832 | tf_op jit(solution)/shard_map/while/body/while/body/eval_jaxpr/cij,cw->ijw/dot_general | solution.py:33
  68.2 1.8 %multiply_convert_fusion.8 = bf16[16,128,128]{2,1,0:T(8,128)(2,1)S(1)} fusion(f32[128,128]{1,0:T(8,128)S(1)} %get-tuple-element.507, f32[16,128]{1,0:T(8,128)S(1)} %dynamic-slice_bitcast_fusion.2, f32[1,16,128]{2,0,1:T(1,128)S(1)} %bitcast.138, f32[3,16,128]{2,0,1:T(4,128)S(1)} %get-tuple-element.481, f32[4,128]{1,0:T(4,128)S(1)} %get-tuple-element.510), kind=kOutput, calls=%fused_computation.6.clone.1 | convolution fusion | flops 14426112 | bytes 632832 | tf_op jit(solution)/shard_map/while/body/while/body/eval_jaxpr/cij,cw->ijw/dot_general | solution.py:33
  71.4 1.8 %multiply_convert_fusion.8 = bf16[16,128,128]{2,1,0:T(8,128)(2,1)S(1)} fusion(f32[128,128]{1,0:T(8,128)S(1)} %get-tuple-element.507, f32[16,128]{1,0:T(8,128)S(1)} %dynamic-slice_bitcast_fusion.2, f32[1,16,128]{2,0,1:T(1,128)S(1)} %bitcast.138, f32[3,16,128]{2,0,1:T(4,128)S(1)} %get-tuple-element.481, f32[4,128]{1,0:T(4,128)S(1)} %get-tuple-element.510), kind=kOutput, calls=%fused_computation.6.clone.1 | convolution fusion | flops 14426112 | bytes 632832 | tf_op jit(solution)/shard_map/while/body/while/body/eval_jaxpr/cij,cw->ijw/dot_general | solution.py:33
  74.6 1.8 %multiply_convert_fusion.8 = bf16[16,128,128]{2,1,0:T(8,128)(2,1)S(1)} fusion(f32[128,128]{1,0:T(8,128)S(1)} %get-tuple-element.507, f32[16,128]{1,0:T(8,128)S(1)} %dynamic-slice_bitcast_fusion.2, f32[1,16,128]{2,0,1:T(1,128)S(1)} %bitcast.138, f32[3,16,128]{2,0,1:T(4,128)S(1)} %get-tuple-element.481, f32[4,128]{1,0:T(4,128)S(1)} %get-tuple-element.510), kind=kOutput, calls=%fused_computation.6.clone.1 | convolution fusion | flops 14426112 | bytes 632832 | tf_op jit(solution)/shard_map/while/body/while/body/eval_jaxpr/cij,cw->ijw/dot_general | solution.py:33
  77.8 1.8 %multiply_convert_fusion.8 = bf16[16,128,128]{2,1,0:T(8,128)(2,1)S(1)} fusion(f32[128,128]{1,0:T(8,128)S(1)} %get-tuple-element.507, f32[16,128]{1,0:T(8,128)S(1)} %dynamic-slice_bitcast_fusion.2, f32[1,16,128]{2,0,1:T(1,128)S(1)} %bitcast.138, f32[3,16,128]{2,0,1:T(4,128)S(1)} %get-tuple-element.481, f32[4,128]{1,0:T(4,128)S(1)} %get-tuple-element.510), kind=kOutput, calls=%fused_computation.6.clone.1 | convolution fusion | flops 14426112 | bytes 632832 | tf_op jit(solution)/shard_map/while/body/while/body/eval_jaxpr/cij,cw->ijw/dot_general | solution.py:33
  81.0 1.8 %multiply_convert_fusion.8 = bf16[16,128,128]{2,1,0:T(8,128)(2,1)S(1)} fusion(f32[128,128]{1,0:T(8,128)S(1)} %get-tuple-element.507, f32[16,128]{1,0:T(8,128)S(1)} %dynamic-slice_bitcast_fusion.2, f32[1,16,128]{2,0,1:T(1,128)S(1)} %bitcast.138, f32[3,16,128]{2,0,1:T(4,128)S(1)} %get-tuple-element.481, f32[4,128]{1,0:T(4,128)S(1)} %get-tuple-element.510), kind=kOutput, calls=%fused_computation.6.clone.1 | convolution fusion | flops 14426112 | bytes 632832 | tf_op jit(solution)/shard_map/while/body/while/body/eval_jaxpr/cij,cw->ijw/dot_general | solution.py:33
  84.2 1.8 %multiply_convert_fusion.8 = bf16[16,128,128]{2,1,0:T(8,128)(2,1)S(1)} fusion(f32[128,128]{1,0:T(8,128)S(1)} %get-tuple-element.507, f32[16,128]{1,0:T(8,128)S(1)} %dynamic-slice_bitcast_fusion.2, f32[1,16,128]{2,0,1:T(1,128)S(1)} %bitcast.138, f32[3,16,128]{2,0,1:T(4,128)S(1)} %get-tuple-element.481, f32[4,128]{1,0:T(4,128)S(1)} %get-tuple-element.510), kind=kOutput, calls=%fused_computation.6.clone.1 | convolution fusion | flops 14426112 | bytes 632832 | tf_op jit(solution)/shard_map/while/body/while/body/eval_jaxpr/cij,cw->ijw/dot_general | solution.py:33
  87.3 0.7 gather_fusion.1
  88.3 0.7 gather_fusion
  89.9 25.6 %while.24 = (s32[]{:T(128)}, f32[8,16,128]{2,1,0:T(8,128)S(1)}, f32[8,16,128]{2,1,0:T(8,128)S(1)}, f32[128,128]{1,0:T(8,128)S(1)}, f32[3,128]{1,0:T(4,128)S(1)},...) while((s32[]{:T(128)}, f32[8,16,128]{2,1,0:T(8,128)S(1)}, ...), condition=%wide.region_3.3_spmd, body=%wide.region_1.2_spmd.sunk | while | flops 86009856 | bytes 3381177 | solution.py:47
  90.2 1.8 %multiply_convert_fusion.8 = bf16[16,128,128]{2,1,0:T(8,128)(2,1)S(1)} fusion(f32[128,128]{1,0:T(8,128)S(1)} %get-tuple-element.507, f32[16,128]{1,0:T(8,128)S(1)} %dynamic-slice_bitcast_fusion.2, f32[1,16,128]{2,0,1:T(1,128)S(1)} %bitcast.138, f32[3,16,128]{2,0,1:T(4,128)S(1)} %get-tuple-element.481, f32[4,128]{1,0:T(4,128)S(1)} %get-tuple-element.510), kind=kOutput, calls=%fused_computation.6.clone.1 | convolution fusion | flops 14426112 | bytes 632832 | tf_op jit(solution)/shard_map/while/body/while/body/eval_jaxpr/cij,cw->ijw/dot_general | solution.py:33
  93.4 1.8 %multiply_convert_fusion.8 = bf16[16,128,128]{2,1,0:T(8,128)(2,1)S(1)} fusion(f32[128,128]{1,0:T(8,128)S(1)} %get-tuple-element.507, f32[16,128]{1,0:T(8,128)S(1)} %dynamic-slice_bitcast_fusion.2, f32[1,16,128]{2,0,1:T(1,128)S(1)} %bitcast.138, f32[3,16,128]{2,0,1:T(4,128)S(1)} %get-tuple-element.481, f32[4,128]{1,0:T(4,128)S(1)} %get-tuple-element.510), kind=kOutput, calls=%fused_computation.6.clone.1 | convolution fusion | flops 14426112 | bytes 632832 | tf_op jit(solution)/shard_map/while/body/while/body/eval_jaxpr/cij,cw->ijw/dot_general | solution.py:33
  96.6 1.8 %multiply_convert_fusion.8 = bf16[16,128,128]{2,1,0:T(8,128)(2,1)S(1)} fusion(f32[128,128]{1,0:T(8,128)S(1)} %get-tuple-element.507, f32[16,128]{1,0:T(8,128)S(1)} %dynamic-slice_bitcast_fusion.2, f32[1,16,128]{2,0,1:T(1,128)S(1)} %bitcast.138, f32[3,16,128]{2,0,1:T(4,128)S(1)} %get-tuple-element.481, f32[4,128]{1,0:T(4,128)S(1)} %get-tuple-element.510), kind=kOutput, calls=%fused_computation.6.clone.1 | convolution fusion | flops 14426112 | bytes 632832 | tf_op jit(solution)/shard_map/while/body/while/body/eval_jaxpr/cij,cw->ijw/dot_general | solution.py:33
  99.8 1.8 %multiply_convert_fusion.8 = bf16[16,128,128]{2,1,0:T(8,128)(2,1)S(1)} fusion(f32[128,128]{1,0:T(8,128)S(1)} %get-tuple-element.507, f32[16,128]{1,0:T(8,128)S(1)} %dynamic-slice_bitcast_fusion.2, f32[1,16,128]{2,0,1:T(1,128)S(1)} %bitcast.138, f32[3,16,128]{2,0,1:T(4,128)S(1)} %get-tuple-element.481, f32[4,128]{1,0:T(4,128)S(1)} %get-tuple-element.510), kind=kOutput, calls=%fused_computation.6.clone.1 | convolution fusion | flops 14426112 | bytes 632832 | tf_op jit(solution)/shard_map/while/body/while/body/eval_jaxpr/cij,cw->ijw/dot_general | solution.py:33
  103.0 1.8 %multiply_convert_fusion.8 = bf16[16,128,128]{2,1,0:T(8,128)(2,1)S(1)} fusion(f32[128,128]{1,0:T(8,128)S(1)} %get-tuple-element.507, f32[16,128]{1,0:T(8,128)S(1)} %dynamic-slice_bitcast_fusion.2, f32[1,16,128]{2,0,1:T(1,128)S(1)} %bitcast.138, f32[3,16,128]{2,0,1:T(4,128)S(1)} %get-tuple-element.481, f32[4,128]{1,0:T(4,128)S(1)} %get-tuple-element.510), kind=kOutput, calls=%fused_computation.6.clone.1 | convolution fusion | flops 14426112 | bytes 632832 | tf_op jit(solution)/shard_map/while/body/while/body/eval_jaxpr/cij,cw->ijw/dot_general | solution.py:33
  106.2 1.8 %multiply_convert_fusion.8 = bf16[16,128,128]{2,1,0:T(8,128)(2,1)S(1)} fusion(f32[128,128]{1,0:T(8,128)S(1)} %get-tuple-element.507, f32[16,128]{1,0:T(8,128)S(1)} %dynamic-slice_bitcast_fusion.2, f32[1,16,128]{2,0,1:T(1,128)S(1)} %bitcast.138, f32[3,16,128]{2,0,1:T(4,128)S(1)} %get-tuple-element.481, f32[4,128]{1,0:T(4,128)S(1)} %get-tuple-element.510), kind=kOutput, calls=%fused_computation.6.clone.1 | convolution fusion | flops 14426112 | bytes 632832 | tf_op jit(solution)/shard_map/while/body/while/body/eval_jaxpr/cij,cw->ijw/dot_general | solution.py:33
  109.4 1.8 %multiply_convert_fusion.8 = bf16[16,128,128]{2,1,0:T(8,128)(2,1)S(1)} fusion(f32[128,128]{1,0:T(8,128)S(1)} %get-tuple-element.507, f32[16,128]{1,0:T(8,128)S(1)} %dynamic-slice_bitcast_fusion.2, f32[1,16,128]{2,0,1:T(1,128)S(1)} %bitcast.138, f32[3,16,128]{2,0,1:T(4,128)S(1)} %get-tuple-element.481, f32[4,128]{1,0:T(4,128)S(1)} %get-tuple-element.510), kind=kOutput, calls=%fused_computation.6.clone.1 | convolution fusion | flops 14426112 | bytes 632832 | tf_op jit(solution)/shard_map/while/body/while/body/eval_jaxpr/cij,cw->ijw/dot_general | solution.py:33
  112.6 1.8 %multiply_convert_fusion.8 = bf16[16,128,128]{2,1,0:T(8,128)(2,1)S(1)} fusion(f32[128,128]{1,0:T(8,128)S(1)} %get-tuple-element.507, f32[16,128]{1,0:T(8,128)S(1)} %dynamic-slice_bitcast_fusion.2, f32[1,16,128]{2,0,1:T(1,128)S(1)} %bitcast.138, f32[3,16,128]{2,0,1:T(4,128)S(1)} %get-tuple-element.481, f32[4,128]{1,0:T(4,128)S(1)} %get-tuple-element.510), kind=kOutput, calls=%fused_computation.6.clone.1 | convolution fusion | flops 14426112 | bytes 632832 | tf_op jit(solution)/shard_map/while/body/while/body/eval_jaxpr/cij,cw->ijw/dot_general | solution.py:33
  116.0 0.7 copy-done.9
  116.7 0.7 copy.45
  (295 shorter events, 36.1 us)
Async XLA Ops:
  0.0 115.6 %copy-start = (bf16[1,128,128]{2,1,0:T(8,128)(2,1)S(1)}, bf16[1,128,128]{2,1,0:T(8,128)(2,1)}, u32[]{:S(2)}) copy-start(bf16[1,128,128]{2,1,0:T(8,128)(2,1)} %param.30) | copy-start | bytes 98308
  5.9 7.4 %copy-start.6 = (bf16[1,1,1,3,128]{4,3,2,1,0:T(4,128)(2,1)S(1)}, bf16[1,1,1,3,128]{4,3,2,1,0:T(4,128)(2,1)}, u32[]{:S(2)}) copy-start(bf16[1,1,1,3,128]{4,3,2,1,0:T(4,128)(2,1)} %param.19) | copy-start | bytes 2308
  5.9 19.3 %copy-start.5 = (s32[1,1,1,384]{3,2,1,0:T(1,128)S(1)}, s32[1,1,1,384]{3,2,1,0:T(1,128)}, u32[]{:S(2)}) copy-start(s32[1,1,1,384]{3,2,1,0:T(1,128)} %param.20) | copy-start | bytes 4612
  5.9 20.1 %copy-start.3 = (bf16[1,128,128]{2,1,0:T(8,128)(2,1)S(1)}, bf16[1,128,128]{2,1,0:T(8,128)(2,1)}, u32[]{:S(2)}) copy-start(bf16[1,128,128]{2,1,0:T(8,128)(2,1)} %param.28) | copy-start | bytes 98308
  7.9 18.1 %copy-start.2 = (bf16[1,1,1,128,128]{4,3,2,1,0:T(8,128)(2,1)S(1)}, bf16[1,1,1,128,128]{4,3,2,1,0:T(8,128)(2,1)}, u32[]{:S(2)}) copy-start(bf16[1,1,1,128,128]{4,3,2,1,0:T(8,128)(2,1)} %param.18) | copy-start | bytes 98308
  7.9 21.8 %collective-permute-start.2 = (bf16[1,2,2,128,128]{4,3,2,1,0:T(8,128)(2,1)S(1)}, bf16[1,2,2,128,128]{4,3,2,1,0:T(8,128)(2,1)S(1)}, u32[]{:S(2)}, u32[]{:S(2)}) collective-permute-start(bf16[1,2,2,128,128]{4,3,2,1,0:T(8,128)(2,1)S(1)} %all_gather.15), channel_id=1, source_target_pairs={{0,4},{4,8},{8,12},{1,5},{5,9},{9,13},{2,6},{6,10},{10,14},{3,7},{... | collective-permute-start | bytes 393224 | tf_op jit(solution)/shard_map/ppermute | solution.py:16
  12.0 17.7 %collective-permute-start.3 = (bf16[1,2,2,128,128]{4,3,2,1,0:T(8,128)(2,1)S(1)}, bf16[1,2,2,128,128]{4,3,2,1,0:T(8,128)(2,1)S(1)}, u32[]{:S(2)}, u32[]{:S(2)}) collective-permute-start(bf16[1,2,2,128,128]{4,3,2,1,0:T(8,128)(2,1)S(1)} %all_gather.15), channel_id=1, source_target_pairs={{4,0},{8,4},{12,8},{5,1},{9,5},{13,9},{6,2},{10,6},{14,10},{7,3},{... | collective-permute-start | bytes 393224 | tf_op jit(solution)/shard_map/ppermute | solution.py:17
  19.4 8.5 %collective-permute-start = (bf16[1,2,2,3,128]{4,3,2,0,1:T(4,128)(2,1)S(1)}, bf16[1,2,2,3,128]{4,3,2,0,1:T(4,128)(2,1)S(1)}, u32[]{:S(2)}, u32[]{:S(2)}) collective-permute-start(bf16[1,2,2,3,128]{4,3,2,0,1:T(4,128)(2,1)S(1)} %all_gather.13), channel_id=1, source_target_pairs={{0,4},{4,8},{8,12},{1,5},{5,9},{9,13},{2,6},{6,10},{10,14},{3,7},{... | collective-permute-start | bytes 9224 | tf_op jit(solution)/shard_map/ppermute | solution.py:16
  23.9 5.5 %collective-permute-start.1 = (bf16[1,2,2,3,128]{4,3,2,0,1:T(4,128)(2,1)S(1)}, bf16[1,2,2,3,128]{4,3,2,0,1:T(4,128)(2,1)S(1)}, u32[]{:S(2)}, u32[]{:S(2)}) collective-permute-start(bf16[1,2,2,3,128]{4,3,2,0,1:T(4,128)(2,1)S(1)} %all_gather.13), channel_id=1, source_target_pairs={{4,0},{8,4},{12,8},{5,1},{9,5},{13,9},{6,2},{10,6},{14,10},{7,3},{... | collective-permute-start | bytes 9224 | tf_op jit(solution)/shard_map/ppermute | solution.py:17
  25.4 0.7 copy-start.7
  26.1 0.8 copy-start.4
  26.2 0.7 copy-start.8
  29.8 0.8 copy-start.1
  29.8 0.8 copy-start.10
  29.8 0.8 copy-start.12
  30.6 85.0 %copy-start.11 = (bf16[1,128,128]{2,1,0:T(8,128)(2,1)S(1)}, bf16[1,128,128]{2,1,0:T(8,128)(2,1)}, u32[]{:S(2)}) copy-start(bf16[1,128,128]{2,1,0:T(8,128)(2,1)} %param.29) | copy-start | bytes 98308
  116.0 0.7 copy-start.9
where the time goes:
time: 118 us; the launch traced here: 117 us
  matrix products  71.3 us (60%)
  blocking collectives  14 us (12%)
  local copies, waits for them, and re-layouts  11.5 us (10%)
  starting transfers between devices  11.2 us (9%)
  other arithmetic  5.12 us (4%)
  loops' own time  1.81 us (2%)
  waiting for transfers between devices  1.59 us (1%)
    dot_general x24, matrix products, tile_messages(): jnp.einsum('cij,cw->ijw', features, rel_weight, precision=lax.Precision.H...  44.2 us
    dot_general x24, matrix products, tile_messages(): jnp.einsum('ijw,j->iw', message, live_mask, precision=lax.Precision.HIGHEST)  15.6 us
    dot_general x24, matrix products, tile_messages(): jnp.dot(edge_act.reshape(-1, latent_width), w_edge, preferred_element_typ...  10.3 us
    all_gather x2, blocking collectives, widen(): collected = lax.all_gather(field, 'gy', axis=1, tiled=True)  10.2 us
    ppermute x2, starting transfers between devices, extended(): before = lax.ppermute(last, axis, up)  8.62 us
    all_gather x2, blocking collectives, widen(): collected = lax.all_gather(collected, 'gz', axis=2, tiled=True)  3.82 us
    unnamed x28, local copies, waits for them, and re-layouts  3.08 us
    ppermute x2, starting transfers between devices, extended(): after = lax.ppermute(first, axis, down)  2.58 us
  transfers between devices with their start and end apart: 4, of which 1 were waited for; matrix products, arithmetic and copies ran while one was open for 1% of the time, Pallas kernels for 0%

commit v1 on v0

--- a/solution.py
+++ b/solution.py
@@ -61,7 +61,7 @@
 
 
 def widen(field):
-    collected = lax.all_gather(field, "gy", axis=1, tiled=True)
+    collected = jnp.concatenate(lax.all_gather(field, "gy"), axis=1)
     collected = lax.all_gather(collected, "gz", axis=2, tiled=True)
     return extended(collected, (("gx", 0),), 1)
 

time: 118 us -> 118 us (level)
  no operation moved by 1% of the time
where the time goes in v1:
time: 118 us; the launch traced here: 117 us
  matrix products  71.3 us (60%)
  blocking collectives  14 us (12%)
  local copies, waits for them, and re-layouts  11.5 us (10%)
  starting transfers between devices  11.2 us (9%)
  other arithmetic  5.11 us (4%)
  loops' own time  1.81 us (2%)
  waiting for transfers between devices  1.59 us (1%)
    dot_general x24, matrix products, tile_messages(): jnp.einsum('cij,cw->ijw', features, rel_weight, precision=lax.Precision.H...  44.2 us
    dot_general x24, matrix products, tile_messages(): jnp.einsum('ijw,j->iw', message, live_mask, precision=lax.Precision.HIGHEST)  15.6 us
    dot_general x24, matrix products, tile_messages(): jnp.dot(edge_act.reshape(-1, latent_width), w_edge, preferred_element_typ...  10.3 us
    all_gather x2, blocking collectives, widen(): collected = jnp.concatenate(lax.all_gather(field, 'gy'), axis=1)  10.2 us
    ppermute x2, starting transfers between devices, extended(): before = lax.ppermute(last, axis, up)  8.62 us
    all_gather x2, blocking collectives, widen(): collected = lax.all_gather(collected, 'gz', axis=2, tiled=True)  3.82 us
    unnamed x28, local copies, waits for them, and re-layouts  3.07 us
    ppermute x2, starting transfers between devices, extended(): after = lax.ppermute(first, axis, down)  2.58 us
  transfers between devices with their start and end apart: 4, of which 1 were waited for; matrix products, arithmetic and copies ran while one was open for 1% of the time, Pallas kernels for 0%

profile of v1, /device:TPU:0, one launch (start us, length us, event | category | flops | bytes accessed | tf_op | source)
XLA Modules:
  0.0 117.5 jit_solution(3612230980208086968)
XLA Ops:
  0.0 5.9 %all-gather.2 = bf16[2,1,1,128,128]{4,3,2,1,0:T(8,128)(2,1)S(1)} all-gather(bf16[1,1,1,128,128]{4,3,2,1,0:T(8,128)(2,1)} %param.18), channel_id=4, replica_groups=mesh['groups'=2,'gx'=4,'gy'=2,'gz'=2] {'gy'}, dimensions={0}, use_global_device_ids=true | all-gather | bytes 98304 | tf_op jit(solution)/shard_map/all_gather | solution.py:64
  5.9 2.0 %all-gather.3 = bf16[2,2,1,128,128]{4,3,2,1,0:T(8,128)(2,1)S(1)} all-gather(bf16[2,1,1,128,128]{4,3,2,1,0:T(8,128)(2,1)S(1)} %all-gather.2), channel_id=5, replica_groups=mesh['groups'=2,'gx'=4,'gy'=2,'gz'=2] {'gz'}, dimensions={1}, use_global_device_ids=true | all-gather | bytes 196608 | tf_op jit(solution)/shard_map/all_gather | solution.py:65
  7.9 4.1 %collective-permute-start.2 = (bf16[1,2,2,128,128]{4,3,2,1,0:T(8,128)(2,1)S(1)}, bf16[1,2,2,128,128]{4,3,2,1,0:T(8,128)(2,1)S(1)}, u32[]{:S(2)}, u32[]{:S(2)}) collective-permute-start(bf16[1,2,2,128,128]{4,3,2,1,0:T(8,128)(2,1)S(1)} %bitcast.141), channel_id=1, source_target_pairs={{0,4},{4,8},{8,12},{1,5},{5,9},{9,13},{2,6},{6,10},{10,14},{3,7},{... | collective-permute-start | bytes 393224 | tf_op jit(solution)/shard_map/ppermute | solution.py:16
  12.0 1.3 %collective-permute-start.3 = (bf16[1,2,2,128,128]{4,3,2,1,0:T(8,128)(2,1)S(1)}, bf16[1,2,2,128,128]{4,3,2,1,0:T(8,128)(2,1)S(1)}, u32[]{:S(2)}, u32[]{:S(2)}) collective-permute-start(bf16[1,2,2,128,128]{4,3,2,1,0:T(8,128)(2,1)S(1)} %bitcast.142), channel_id=1, source_target_pairs={{4,0},{8,4},{12,8},{5,1},{9,5},{13,9},{6,2},{10,6},{14,10},{7,3},{... | collective-permute-start | bytes 393224 | tf_op jit(solution)/shard_map/ppermute | solution.py:17
  13.4 4.2 %all-gather = bf16[2,1,1,3,128]{4,3,2,1,0:T(4,128)(2,1)S(1)} all-gather(bf16[1,1,1,3,128]{4,3,2,1,0:T(4,128)(2,1)S(1)} %copy-done.6), channel_id=2, replica_groups=mesh['groups'=2,'gx'=4,'gy'=2,'gz'=2] {'gy'}, dimensions={0}, use_global_device_ids=true | all-gather | bytes 2304 | tf_op jit(solution)/shard_map/all_gather | solution.py:64
  17.6 1.8 %all-gather.1 = bf16[2,2,1,3,128]{4,3,2,1,0:T(4,128)(2,1)S(1)} all-gather(bf16[2,1,1,3,128]{4,3,2,1,0:T(4,128)(2,1)S(1)} %all-gather), channel_id=3, replica_groups=mesh['groups'=2,'gx'=4,'gy'=2,'gz'=2] {'gz'}, dimensions={1}, use_global_device_ids=true | all-gather | bytes 4608 | tf_op jit(solution)/shard_map/all_gather | solution.py:65
  19.4 4.5 %collective-permute-start = (bf16[1,2,2,3,128]{4,3,2,1,0:T(4,128)(2,1)S(1)}, bf16[1,2,2,3,128]{4,3,2,1,0:T(4,128)(2,1)S(1)}, u32[]{:S(2)}, u32[]{:S(2)}) collective-permute-start(bf16[1,2,2,3,128]{4,3,2,1,0:T(4,128)(2,1)S(1)} %bitcast.145), channel_id=1, source_target_pairs={{0,4},{4,8},{8,12},{1,5},{5,9},{9,13},{2,6},{6,10},{10,14},{3,7},{... | collective-permute-start | bytes 9224 | tf_op jit(solution)/shard_map/ppermute | solution.py:16
  23.9 1.3 %collective-permute-start.1 = (bf16[1,2,2,3,128]{4,3,2,1,0:T(4,128)(2,1)S(1)}, bf16[1,2,2,3,128]{4,3,2,1,0:T(4,128)(2,1)S(1)}, u32[]{:S(2)}, u32[]{:S(2)}) collective-permute-start(bf16[1,2,2,3,128]{4,3,2,1,0:T(4,128)(2,1)S(1)} %bitcast.146), channel_id=1, source_target_pairs={{4,0},{8,4},{12,8},{5,1},{9,5},{13,9},{6,2},{10,6},{14,10},{7,3},{... | collective-permute-start | bytes 9224 | tf_op jit(solution)/shard_map/ppermute | solution.py:17
  27.9 1.6 %collective-permute-done.1 = bf16[1,2,2,3,128]{4,3,2,1,0:T(4,128)(2,1)S(1)} collective-permute-done((bf16[1,2,2,3,128]{4,3,2,1,0:T(4,128)(2,1)S(1)}, bf16[1,2,2,3,128]{4,3,2,1,0:T(4,128)(2,1)S(1)}, u32[]{:S(2)}, u32[]{:S(2)}) %collective-permute-start.1) | collective-permute-done | bytes 3104 | tf_op jit(solution)/shard_map/ppermute | solution.py:17
  29.8 0.7 copy-done.1
  30.6 85.0 %while.23 = (s32[]{:T(128)}, f32[128,128]{1,0:T(8,128)S(1)}, s32[]{:T(128)}, f32[128,128]{1,0:T(8,128)S(1)}, f32[1,1,1,3,128]{4,3,2,1,0:T(4,128)S(1)}, /*index=5...) while((s32[]{:T(128)}, f32[128,128]{1,0:T(8,128)S(1)}, ...), condition=%wide.region_4.5_spmd.clone, body=%wide.region_0.4_spmd.clone.sunk | while | flops 90240648 | bytes 3800472 | solution.py:158
  30.6 0.7 gather_fusion.1
  31.6 0.7 gather_fusion
  32.5 0.7 compare_convert_fusion.2
  33.3 25.6 %while.24 = (s32[]{:T(128)}, f32[8,16,128]{2,1,0:T(8,128)S(1)}, f32[8,16,128]{2,1,0:T(8,128)S(1)}, f32[128,128]{1,0:T(8,128)S(1)}, f32[3,128]{1,0:T(4,128)S(1)},...) while((s32[]{:T(128)}, f32[8,16,128]{2,1,0:T(8,128)S(1)}, ...), condition=%wide.region_3.3_spmd, body=%wide.region_1.2_spmd.sunk | while | flops 86009856 | bytes 3381177 | solution.py:47
  33.5 1.8 %multiply_convert_fusion.8 = bf16[16,128,128]{2,1,0:T(8,128)(2,1)S(1)} fusion(f32[128,128]{1,0:T(8,128)S(1)} %get-tuple-element.507, f32[16,128]{1,0:T(8,128)S(1)} %dynamic-slice_bitcast_fusion.2, f32[1,16,128]{2,0,1:T(1,128)S(1)} %bitcast.137, f32[3,16,128]{2,0,1:T(4,128)S(1)} %get-tuple-element.481, f32[4,128]{1,0:T(4,128)S(1)} %get-tuple-element.510), kind=kOutput, calls=%fused_computation.6.clone.1 | convolution fusion | flops 14426112 | bytes 632832 | tf_op jit(solution)/shard_map/while/body/while/body/eval_jaxpr/cij,cw->ijw/dot_general | solution.py:33
  36.7 1.8 %multiply_convert_fusion.8 = bf16[16,128,128]{2,1,0:T(8,128)(2,1)S(1)} fusion(f32[128,128]{1,0:T(8,128)S(1)} %get-tuple-element.507, f32[16,128]{1,0:T(8,128)S(1)} %dynamic-slice_bitcast_fusion.2, f32[1,16,128]{2,0,1:T(1,128)S(1)} %bitcast.137, f32[3,16,128]{2,0,1:T(4,128)S(1)} %get-tuple-element.481, f32[4,128]{1,0:T(4,128)S(1)} %get-tuple-element.510), kind=kOutput, calls=%fused_computation.6.clone.1 | convolution fusion | flops 14426112 | bytes 632832 | tf_op jit(solution)/shard_map/while/body/while/body/eval_jaxpr/cij,cw->ijw/dot_general | solution.py:33
  39.9 1.8 %multiply_convert_fusion.8 = bf16[16,128,128]{2,1,0:T(8,128)(2,1)S(1)} fusion(f32[128,128]{1,0:T(8,128)S(1)} %get-tuple-element.507, f32[16,128]{1,0:T(8,128)S(1)} %dynamic-slice_bitcast_fusion.2, f32[1,16,128]{2,0,1:T(1,128)S(1)} %bitcast.137, f32[3,16,128]{2,0,1:T(4,128)S(1)} %get-tuple-element.481, f32[4,128]{1,0:T(4,128)S(1)} %get-tuple-element.510), kind=kOutput, calls=%fused_computation.6.clone.1 | convolution fusion | flops 14426112 | bytes 632832 | tf_op jit(solution)/shard_map/while/body/while/body/eval_jaxpr/cij,cw->ijw/dot_general | solution.py:33
  43.1 1.8 %multiply_convert_fusion.8 = bf16[16,128,128]{2,1,0:T(8,128)(2,1)S(1)} fusion(f32[128,128]{1,0:T(8,128)S(1)} %get-tuple-element.507, f32[16,128]{1,0:T(8,128)S(1)} %dynamic-slice_bitcast_fusion.2, f32[1,16,128]{2,0,1:T(1,128)S(1)} %bitcast.137, f32[3,16,128]{2,0,1:T(4,128)S(1)} %get-tuple-element.481, f32[4,128]{1,0:T(4,128)S(1)} %get-tuple-element.510), kind=kOutput, calls=%fused_computation.6.clone.1 | convolution fusion | flops 14426112 | bytes 632832 | tf_op jit(solution)/shard_map/while/body/while/body/eval_jaxpr/cij,cw->ijw/dot_general | solution.py:33
  46.3 1.8 %multiply_convert_fusion.8 = bf16[16,128,128]{2,1,0:T(8,128)(2,1)S(1)} fusion(f32[128,128]{1,0:T(8,128)S(1)} %get-tuple-element.507, f32[16,128]{1,0:T(8,128)S(1)} %dynamic-slice_bitcast_fusion.2, f32[1,16,128]{2,0,1:T(1,128)S(1)} %bitcast.137, f32[3,16,128]{2,0,1:T(4,128)S(1)} %get-tuple-element.481, f32[4,128]{1,0:T(4,128)S(1)} %get-tuple-element.510), kind=kOutput, calls=%fused_computation.6.clone.1 | convolution fusion | flops 14426112 | bytes 632832 | tf_op jit(solution)/shard_map/while/body/while/body/eval_jaxpr/cij,cw->ijw/dot_general | solution.py:33
  49.5 1.8 %multiply_convert_fusion.8 = bf16[16,128,128]{2,1,0:T(8,128)(2,1)S(1)} fusion(f32[128,128]{1,0:T(8,128)S(1)} %get-tuple-element.507, f32[16,128]{1,0:T(8,128)S(1)} %dynamic-slice_bitcast_fusion.2, f32[1,16,128]{2,0,1:T(1,128)S(1)} %bitcast.137, f32[3,16,128]{2,0,1:T(4,128)S(1)} %get-tuple-element.481, f32[4,128]{1,0:T(4,128)S(1)} %get-tuple-element.510), kind=kOutput, calls=%fused_computation.6.clone.1 | convolution fusion | flops 14426112 | bytes 632832 | tf_op jit(solution)/shard_map/while/body/while/body/eval_jaxpr/cij,cw->ijw/dot_general | solution.py:33
  52.7 1.8 %multiply_convert_fusion.8 = bf16[16,128,128]{2,1,0:T(8,128)(2,1)S(1)} fusion(f32[128,128]{1,0:T(8,128)S(1)} %get-tuple-element.507, f32[16,128]{1,0:T(8,128)S(1)} %dynamic-slice_bitcast_fusion.2, f32[1,16,128]{2,0,1:T(1,128)S(1)} %bitcast.137, f32[3,16,128]{2,0,1:T(4,128)S(1)} %get-tuple-element.481, f32[4,128]{1,0:T(4,128)S(1)} %get-tuple-element.510), kind=kOutput, calls=%fused_computation.6.clone.1 | convolution fusion | flops 14426112 | bytes 632832 | tf_op jit(solution)/shard_map/while/body/while/body/eval_jaxpr/cij,cw->ijw/dot_general | solution.py:33
  55.9 1.8 %multiply_convert_fusion.8 = bf16[16,128,128]{2,1,0:T(8,128)(2,1)S(1)} fusion(f32[128,128]{1,0:T(8,128)S(1)} %get-tuple-element.507, f32[16,128]{1,0:T(8,128)S(1)} %dynamic-slice_bitcast_fusion.2, f32[1,16,128]{2,0,1:T(1,128)S(1)} %bitcast.137, f32[3,16,128]{2,0,1:T(4,128)S(1)} %get-tuple-element.481, f32[4,128]{1,0:T(4,128)S(1)} %get-tuple-element.510), kind=kOutput, calls=%fused_computation.6.clone.1 | convolution fusion | flops 14426112 | bytes 632832 | tf_op jit(solution)/shard_map/while/body/while/body/eval_jaxpr/cij,cw->ijw/dot_general | solution.py:33
  58.9 0.7 gather_fusion.1
  60.0 0.7 gather_fusion
  60.9 0.7 compare_convert_fusion.2
  61.6 25.6 %while.24 = (s32[]{:T(128)}, f32[8,16,128]{2,1,0:T(8,128)S(1)}, f32[8,16,128]{2,1,0:T(8,128)S(1)}, f32[128,128]{1,0:T(8,128)S(1)}, f32[3,128]{1,0:T(4,128)S(1)},...) while((s32[]{:T(128)}, f32[8,16,128]{2,1,0:T(8,128)S(1)}, ...), condition=%wide.region_3.3_spmd, body=%wide.region_1.2_spmd.sunk | while | flops 86009856 | bytes 3381177 | solution.py:47
  61.9 1.8 %multiply_convert_fusion.8 = bf16[16,128,128]{2,1,0:T(8,128)(2,1)S(1)} fusion(f32[128,128]{1,0:T(8,128)S(1)} %get-tuple-element.507, f32[16,128]{1,0:T(8,128)S(1)} %dynamic-slice_bitcast_fusion.2, f32[1,16,128]{2,0,1:T(1,128)S(1)} %bitcast.137, f32[3,16,128]{2,0,1:T(4,128)S(1)} %get-tuple-element.481, f32[4,128]{1,0:T(4,128)S(1)} %get-tuple-element.510), kind=kOutput, calls=%fused_computation.6.clone.1 | convolution fusion | flops 14426112 | bytes 632832 | tf_op jit(solution)/shard_map/while/body/while/body/eval_jaxpr/cij,cw->ijw/dot_general | solution.py:33
  65.1 1.8 %multiply_convert_fusion.8 = bf16[16,128,128]{2,1,0:T(8,128)(2,1)S(1)} fusion(f32[128,128]{1,0:T(8,128)S(1)} %get-tuple-element.507, f32[16,128]{1,0:T(8,128)S(1)} %dynamic-slice_bitcast_fusion.2, f32[1,16,128]{2,0,1:T(1,128)S(1)} %bitcast.137, f32[3,16,128]{2,0,1:T(4,128)S(1)} %get-tuple-element.481, f32[4,128]{1,0:T(4,128)S(1)} %get-tuple-element.510), kind=kOutput, calls=%fused_computation.6.clone.1 | convolution fusion | flops 14426112 | bytes 632832 | tf_op jit(solution)/shard_map/while/body/while/body/eval_jaxpr/cij,cw->ijw/dot_general | solution.py:33
  68.3 1.8 %multiply_convert_fusion.8 = bf16[16,128,128]{2,1,0:T(8,128)(2,1)S(1)} fusion(f32[128,128]{1,0:T(8,128)S(1)} %get-tuple-element.507, f32[16,128]{1,0:T(8,128)S(1)} %dynamic-slice_bitcast_fusion.2, f32[1,16,128]{2,0,1:T(1,128)S(1)} %bitcast.137, f32[3,16,128]{2,0,1:T(4,128)S(1)} %get-tuple-element.481, f32[4,128]{1,0:T(4,128)S(1)} %get-tuple-element.510), kind=kOutput, calls=%fused_computation.6.clone.1 | convolution fusion | flops 14426112 | bytes 632832 | tf_op jit(solution)/shard_map/while/body/while/body/eval_jaxpr/cij,cw->ijw/dot_general | solution.py:33
  71.5 1.8 %multiply_convert_fusion.8 = bf16[16,128,128]{2,1,0:T(8,128)(2,1)S(1)} fusion(f32[128,128]{1,0:T(8,128)S(1)} %get-tuple-element.507, f32[16,128]{1,0:T(8,128)S(1)} %dynamic-slice_bitcast_fusion.2, f32[1,16,128]{2,0,1:T(1,128)S(1)} %bitcast.137, f32[3,16,128]{2,0,1:T(4,128)S(1)} %get-tuple-element.481, f32[4,128]{1,0:T(4,128)S(1)} %get-tuple-element.510), kind=kOutput, calls=%fused_computation.6.clone.1 | convolution fusion | flops 14426112 | bytes 632832 | tf_op jit(solution)/shard_map/while/body/while/body/eval_jaxpr/cij,cw->ijw/dot_general | solution.py:33
  74.7 1.8 %multiply_convert_fusion.8 = bf16[16,128,128]{2,1,0:T(8,128)(2,1)S(1)} fusion(f32[128,128]{1,0:T(8,128)S(1)} %get-tuple-element.507, f32[16,128]{1,0:T(8,128)S(1)} %dynamic-slice_bitcast_fusion.2, f32[1,16,128]{2,0,1:T(1,128)S(1)} %bitcast.137, f32[3,16,128]{2,0,1:T(4,128)S(1)} %get-tuple-element.481, f32[4,128]{1,0:T(4,128)S(1)} %get-tuple-element.510), kind=kOutput, calls=%fused_computation.6.clone.1 | convolution fusion | flops 14426112 | bytes 632832 | tf_op jit(solution)/shard_map/while/body/while/body/eval_jaxpr/cij,cw->ijw/dot_general | solution.py:33
  77.9 1.8 %multiply_convert_fusion.8 = bf16[16,128,128]{2,1,0:T(8,128)(2,1)S(1)} fusion(f32[128,128]{1,0:T(8,128)S(1)} %get-tuple-element.507, f32[16,128]{1,0:T(8,128)S(1)} %dynamic-slice_bitcast_fusion.2, f32[1,16,128]{2,0,1:T(1,128)S(1)} %bitcast.137, f32[3,16,128]{2,0,1:T(4,128)S(1)} %get-tuple-element.481, f32[4,128]{1,0:T(4,128)S(1)} %get-tuple-element.510), kind=kOutput, calls=%fused_computation.6.clone.1 | convolution fusion | flops 14426112 | bytes 632832 | tf_op jit(solution)/shard_map/while/body/while/body/eval_jaxpr/cij,cw->ijw/dot_general | solution.py:33
  81.1 1.8 %multiply_convert_fusion.8 = bf16[16,128,128]{2,1,0:T(8,128)(2,1)S(1)} fusion(f32[128,128]{1,0:T(8,128)S(1)} %get-tuple-element.507, f32[16,128]{1,0:T(8,128)S(1)} %dynamic-slice_bitcast_fusion.2, f32[1,16,128]{2,0,1:T(1,128)S(1)} %bitcast.137, f32[3,16,128]{2,0,1:T(4,128)S(1)} %get-tuple-element.481, f32[4,128]{1,0:T(4,128)S(1)} %get-tuple-element.510), kind=kOutput, calls=%fused_computation.6.clone.1 | convolution fusion | flops 14426112 | bytes 632832 | tf_op jit(solution)/shard_map/while/body/while/body/eval_jaxpr/cij,cw->ijw/dot_general | solution.py:33
  84.3 1.8 %multiply_convert_fusion.8 = bf16[16,128,128]{2,1,0:T(8,128)(2,1)S(1)} fusion(f32[128,128]{1,0:T(8,128)S(1)} %get-tuple-element.507, f32[16,128]{1,0:T(8,128)S(1)} %dynamic-slice_bitcast_fusion.2, f32[1,16,128]{2,0,1:T(1,128)S(1)} %bitcast.137, f32[3,16,128]{2,0,1:T(4,128)S(1)} %get-tuple-element.481, f32[4,128]{1,0:T(4,128)S(1)} %get-tuple-element.510), kind=kOutput, calls=%fused_computation.6.clone.1 | convolution fusion | flops 14426112 | bytes 632832 | tf_op jit(solution)/shard_map/while/body/while/body/eval_jaxpr/cij,cw->ijw/dot_general | solution.py:33
  87.3 0.7 gather_fusion.1
  88.3 0.7 gather_fusion
  90.0 25.6 %while.24 = (s32[]{:T(128)}, f32[8,16,128]{2,1,0:T(8,128)S(1)}, f32[8,16,128]{2,1,0:T(8,128)S(1)}, f32[128,128]{1,0:T(8,128)S(1)}, f32[3,128]{1,0:T(4,128)S(1)},...) while((s32[]{:T(128)}, f32[8,16,128]{2,1,0:T(8,128)S(1)}, ...), condition=%wide.region_3.3_spmd, body=%wide.region_1.2_spmd.sunk | while | flops 86009856 | bytes 3381177 | solution.py:47
  90.2 1.8 %multiply_convert_fusion.8 = bf16[16,128,128]{2,1,0:T(8,128)(2,1)S(1)} fusion(f32[128,128]{1,0:T(8,128)S(1)} %get-tuple-element.507, f32[16,128]{1,0:T(8,128)S(1)} %dynamic-slice_bitcast_fusion.2, f32[1,16,128]{2,0,1:T(1,128)S(1)} %bitcast.137, f32[3,16,128]{2,0,1:T(4,128)S(1)} %get-tuple-element.481, f32[4,128]{1,0:T(4,128)S(1)} %get-tuple-element.510), kind=kOutput, calls=%fused_computation.6.clone.1 | convolution fusion | flops 14426112 | bytes 632832 | tf_op jit(solution)/shard_map/while/body/while/body/eval_jaxpr/cij,cw->ijw/dot_general | solution.py:33
  93.4 1.8 %multiply_convert_fusion.8 = bf16[16,128,128]{2,1,0:T(8,128)(2,1)S(1)} fusion(f32[128,128]{1,0:T(8,128)S(1)} %get-tuple-element.507, f32[16,128]{1,0:T(8,128)S(1)} %dynamic-slice_bitcast_fusion.2, f32[1,16,128]{2,0,1:T(1,128)S(1)} %bitcast.137, f32[3,16,128]{2,0,1:T(4,128)S(1)} %get-tuple-element.481, f32[4,128]{1,0:T(4,128)S(1)} %get-tuple-element.510), kind=kOutput, calls=%fused_computation.6.clone.1 | convolution fusion | flops 14426112 | bytes 632832 | tf_op jit(solution)/shard_map/while/body/while/body/eval_jaxpr/cij,cw->ijw/dot_general | solution.py:33
  96.6 1.8 %multiply_convert_fusion.8 = bf16[16,128,128]{2,1,0:T(8,128)(2,1)S(1)} fusion(f32[128,128]{1,0:T(8,128)S(1)} %get-tuple-element.507, f32[16,128]{1,0:T(8,128)S(1)} %dynamic-slice_bitcast_fusion.2, f32[1,16,128]{2,0,1:T(1,128)S(1)} %bitcast.137, f32[3,16,128]{2,0,1:T(4,128)S(1)} %get-tuple-element.481, f32[4,128]{1,0:T(4,128)S(1)} %get-tuple-element.510), kind=kOutput, calls=%fused_computation.6.clone.1 | convolution fusion | flops 14426112 | bytes 632832 | tf_op jit(solution)/shard_map/while/body/while/body/eval_jaxpr/cij,cw->ijw/dot_general | solution.py:33
  99.8 1.8 %multiply_convert_fusion.8 = bf16[16,128,128]{2,1,0:T(8,128)(2,1)S(1)} fusion(f32[128,128]{1,0:T(8,128)S(1)} %get-tuple-element.507, f32[16,128]{1,0:T(8,128)S(1)} %dynamic-slice_bitcast_fusion.2, f32[1,16,128]{2,0,1:T(1,128)S(1)} %bitcast.137, f32[3,16,128]{2,0,1:T(4,128)S(1)} %get-tuple-element.481, f32[4,128]{1,0:T(4,128)S(1)} %get-tuple-element.510), kind=kOutput, calls=%fused_computation.6.clone.1 | convolution fusion | flops 14426112 | bytes 632832 | tf_op jit(solution)/shard_map/while/body/while/body/eval_jaxpr/cij,cw->ijw/dot_general | solution.py:33
  103.0 1.8 %multiply_convert_fusion.8 = bf16[16,128,128]{2,1,0:T(8,128)(2,1)S(1)} fusion(f32[128,128]{1,0:T(8,128)S(1)} %get-tuple-element.507, f32[16,128]{1,0:T(8,128)S(1)} %dynamic-slice_bitcast_fusion.2, f32[1,16,128]{2,0,1:T(1,128)S(1)} %bitcast.137, f32[3,16,128]{2,0,1:T(4,128)S(1)} %get-tuple-element.481, f32[4,128]{1,0:T(4,128)S(1)} %get-tuple-element.510), kind=kOutput, calls=%fused_computation.6.clone.1 | convolution fusion | flops 14426112 | bytes 632832 | tf_op jit(solution)/shard_map/while/body/while/body/eval_jaxpr/cij,cw->ijw/dot_general | solution.py:33
  106.2 1.8 %multiply_convert_fusion.8 = bf16[16,128,128]{2,1,0:T(8,128)(2,1)S(1)} fusion(f32[128,128]{1,0:T(8,128)S(1)} %get-tuple-element.507, f32[16,128]{1,0:T(8,128)S(1)} %dynamic-slice_bitcast_fusion.2, f32[1,16,128]{2,0,1:T(1,128)S(1)} %bitcast.137, f32[3,16,128]{2,0,1:T(4,128)S(1)} %get-tuple-element.481, f32[4,128]{1,0:T(4,128)S(1)} %get-tuple-element.510), kind=kOutput, calls=%fused_computation.6.clone.1 | convolution fusion | flops 14426112 | bytes 632832 | tf_op jit(solution)/shard_map/while/body/while/body/eval_jaxpr/cij,cw->ijw/dot_general | solution.py:33
  109.4 1.8 %multiply_convert_fusion.8 = bf16[16,128,128]{2,1,0:T(8,128)(2,1)S(1)} fusion(f32[128,128]{1,0:T(8,128)S(1)} %get-tuple-element.507, f32[16,128]{1,0:T(8,128)S(1)} %dynamic-slice_bitcast_fusion.2, f32[1,16,128]{2,0,1:T(1,128)S(1)} %bitcast.137, f32[3,16,128]{2,0,1:T(4,128)S(1)} %get-tuple-element.481, f32[4,128]{1,0:T(4,128)S(1)} %get-tuple-element.510), kind=kOutput, calls=%fused_computation.6.clone.1 | convolution fusion | flops 14426112 | bytes 632832 | tf_op jit(solution)/shard_map/while/body/while/body/eval_jaxpr/cij,cw->ijw/dot_general | solution.py:33
  112.6 1.8 %multiply_convert_fusion.8 = bf16[16,128,128]{2,1,0:T(8,128)(2,1)S(1)} fusion(f32[128,128]{1,0:T(8,128)S(1)} %get-tuple-element.507, f32[16,128]{1,0:T(8,128)S(1)} %dynamic-slice_bitcast_fusion.2, f32[1,16,128]{2,0,1:T(1,128)S(1)} %bitcast.137, f32[3,16,128]{2,0,1:T(4,128)S(1)} %get-tuple-element.481, f32[4,128]{1,0:T(4,128)S(1)} %get-tuple-element.510), kind=kOutput, calls=%fused_computation.6.clone.1 | convolution fusion | flops 14426112 | bytes 632832 | tf_op jit(solution)/shard_map/while/body/while/body/eval_jaxpr/cij,cw->ijw/dot_general | solution.py:33
  116.0 0.7 copy-done.9
  116.7 0.7 copy.39
  (295 shorter events, 36.1 us)
Async XLA Ops:
  0.0 115.6 %copy-start = (bf16[1,128,128]{2,1,0:T(8,128)(2,1)S(1)}, bf16[1,128,128]{2,1,0:T(8,128)(2,1)}, u32[]{:S(2)}) copy-start(bf16[1,128,128]{2,1,0:T(8,128)(2,1)} %param.30) | copy-start | bytes 98308
  5.9 7.4 %copy-start.6 = (bf16[1,1,1,3,128]{4,3,2,1,0:T(4,128)(2,1)S(1)}, bf16[1,1,1,3,128]{4,3,2,1,0:T(4,128)(2,1)}, u32[]{:S(2)}) copy-start(bf16[1,1,1,3,128]{4,3,2,1,0:T(4,128)(2,1)} %param.19) | copy-start | bytes 2308
  5.9 19.3 %copy-start.5 = (s32[1,1,1,384]{3,2,1,0:T(1,128)S(1)}, s32[1,1,1,384]{3,2,1,0:T(1,128)}, u32[]{:S(2)}) copy-start(s32[1,1,1,384]{3,2,1,0:T(1,128)} %param.20) | copy-start | bytes 4612
  5.9 20.1 %copy-start.3 = (bf16[1,128,128]{2,1,0:T(8,128)(2,1)S(1)}, bf16[1,128,128]{2,1,0:T(8,128)(2,1)}, u32[]{:S(2)}) copy-start(bf16[1,128,128]{2,1,0:T(8,128)(2,1)} %param.28) | copy-start | bytes 98308
  7.9 18.1 %copy-start.2 = (bf16[1,1,1,128,128]{4,3,2,1,0:T(8,128)(2,1)S(1)}, bf16[1,1,1,128,128]{4,3,2,1,0:T(8,128)(2,1)}, u32[]{:S(2)}) copy-start(bf16[1,1,1,128,128]{4,3,2,1,0:T(8,128)(2,1)} %param.18) | copy-start | bytes 98308
  7.9 21.8 %collective-permute-start.2 = (bf16[1,2,2,128,128]{4,3,2,1,0:T(8,128)(2,1)S(1)}, bf16[1,2,2,128,128]{4,3,2,1,0:T(8,128)(2,1)S(1)}, u32[]{:S(2)}, u32[]{:S(2)}) collective-permute-start(bf16[1,2,2,128,128]{4,3,2,1,0:T(8,128)(2,1)S(1)} %bitcast.141), channel_id=1, source_target_pairs={{0,4},{4,8},{8,12},{1,5},{5,9},{9,13},{2,6},{6,10},{10,14},{3,7},{... | collective-permute-start | bytes 393224 | tf_op jit(solution)/shard_map/ppermute | solution.py:16
  12.0 17.7 %collective-permute-start.3 = (bf16[1,2,2,128,128]{4,3,2,1,0:T(8,128)(2,1)S(1)}, bf16[1,2,2,128,128]{4,3,2,1,0:T(8,128)(2,1)S(1)}, u32[]{:S(2)}, u32[]{:S(2)}) collective-permute-start(bf16[1,2,2,128,128]{4,3,2,1,0:T(8,128)(2,1)S(1)} %bitcast.142), channel_id=1, source_target_pairs={{4,0},{8,4},{12,8},{5,1},{9,5},{13,9},{6,2},{10,6},{14,10},{7,3},{... | collective-permute-start | bytes 393224 | tf_op jit(solution)/shard_map/ppermute | solution.py:17
  19.4 8.5 %collective-permute-start = (bf16[1,2,2,3,128]{4,3,2,1,0:T(4,128)(2,1)S(1)}, bf16[1,2,2,3,128]{4,3,2,1,0:T(4,128)(2,1)S(1)}, u32[]{:S(2)}, u32[]{:S(2)}) collective-permute-start(bf16[1,2,2,3,128]{4,3,2,1,0:T(4,128)(2,1)S(1)} %bitcast.145), channel_id=1, source_target_pairs={{0,4},{4,8},{8,12},{1,5},{5,9},{9,13},{2,6},{6,10},{10,14},{3,7},{... | collective-permute-start | bytes 9224 | tf_op jit(solution)/shard_map/ppermute | solution.py:16
  23.9 5.5 %collective-permute-start.1 = (bf16[1,2,2,3,128]{4,3,2,1,0:T(4,128)(2,1)S(1)}, bf16[1,2,2,3,128]{4,3,2,1,0:T(4,128)(2,1)S(1)}, u32[]{:S(2)}, u32[]{:S(2)}) collective-permute-start(bf16[1,2,2,3,128]{4,3,2,1,0:T(4,128)(2,1)S(1)} %bitcast.146), channel_id=1, source_target_pairs={{4,0},{8,4},{12,8},{5,1},{9,5},{13,9},{6,2},{10,6},{14,10},{7,3},{... | collective-permute-start | bytes 9224 | tf_op jit(solution)/shard_map/ppermute | solution.py:17
  25.4 0.7 copy-start.7
  26.1 0.8 copy-start.4
  26.2 0.7 copy-start.8
  29.8 0.8 copy-start.1
  29.8 0.8 copy-start.10
  29.8 0.8 copy-start.12
  30.6 85.0 %copy-start.11 = (bf16[1,128,128]{2,1,0:T(8,128)(2,1)S(1)}, bf16[1,128,128]{2,1,0:T(8,128)(2,1)}, u32[]{:S(2)}) copy-start(bf16[1,128,128]{2,1,0:T(8,128)(2,1)} %param.29) | copy-start | bytes 98308
  116.0 0.7 copy-start.9
